TPU v7x, 256 devices: a whole 4x4x8 slice. The times are simulated.
256 devices in a mesh: prow: 16 (over x, y), pcol: 16 (over z, core).
Axes of the slice: x: 4, y: 4, z: 8, core: 2. Of those that a mesh axis runs over, the one named last changes fastest.
Arguments:
- matrix: float32 [16384, 16384], P('prow', 'pcol'), may hold values from -6 to 6
- pivots: int32 [2, 512], replicated, may hold values from 512 to 16383, as said below
- lower_inverses: float32 [2, 512, 512], replicated, as said below
- upper_inverses: float32 [2, 512, 512], replicated, as said below
Outputs:
- factored: float32 [16384, 16384], P('prow', 'pcol')
Inputs may be any that keep to these rules, and one draw needn't show every extreme that they name: The 512 entries of pivots[j] are distinct and each is at least (j + 1) * 512. Each lower_inverses[j] is unit lower triangular. Each upper_inverses[j] is upper triangular with a positive diagonal.
All inputs are finite; a program needn't handle non-finite values.
Results may differ from a plain program's by a relative error of at most 0.0003.
Values sent between devices are 32-bit elements; how exact they have to be, the bound alone decides.
A program may use at most 128 MiB of HBM per device.

v0:
```python
import jax
import jax.numpy as jnp
from jax import lax
from jax.sharding import PartitionSpec as P


def spread(value, axis, source):
    kept = jnp.where(lax.axis_index(axis) == source, value, 0).astype(value.dtype)
    return lax.psum(kept, axis)


def body(matrix, pivots, lower_inverses, upper_inverses):
    row_count = lax.axis_size("prow")
    col_count = lax.axis_size("pcol")
    my_row = lax.axis_index("prow")
    my_col = lax.axis_index("pcol")
    rows_local, cols_local = matrix.shape
    panel_width = lower_inverses.shape[1]
    row_blocks = jnp.arange(rows_local, dtype=jnp.int32) // panel_width * row_count + my_row
    col_blocks = jnp.arange(cols_local, dtype=jnp.int32) // panel_width * col_count + my_col
    current = matrix
    for panel_step in range(pivots.shape[0]):
        targets = pivots[panel_step]
        global_blocks = targets // panel_width
        owner_row = global_blocks % row_count
        local_slot = global_blocks // row_count * panel_width + targets % panel_width
        is_mine = owner_row == my_row
        picked = jnp.where(is_mine[:, None], current[local_slot], 0.0)
        old_top = spread(current[:panel_width], "prow", panel_step)
        inverse_lower = lower_inverses[panel_step]
        new_top = lax.psum(picked, "prow")
        formed = jnp.dot(
            inverse_lower,
            new_top,
            precision=lax.Precision.HIGHEST,
            preferred_element_type=jnp.float32,
        )
        top_rows = jnp.where((col_blocks > panel_step)[None, :], formed, new_top)
        dropped_slot = jnp.where(is_mine, local_slot, rows_local)
        current = current.at[dropped_slot].set(old_top, mode="drop")
        on_diagonal = my_row == panel_step
        current = current.at[:panel_width].set(
            jnp.where(on_diagonal, top_rows, current[:panel_width])
        )
        column = spread(current[:, :panel_width], "pcol", panel_step)
        lower_full = jnp.dot(
            column,
            upper_inverses[panel_step],
            precision=lax.Precision.HIGHEST,
            preferred_element_type=jnp.float32,
        )
        is_below = (row_blocks > panel_step)[:, None]
        lower_part = jnp.where(is_below, lower_full, 0.0)
        upper_part = jnp.where((col_blocks > panel_step)[None, :], top_rows, 0.0)
        current = current - jnp.dot(
            lower_part,
            upper_part,
            precision=lax.Precision.HIGHEST,
            preferred_element_type=jnp.float32,
        )
        current = current.at[:, :panel_width].set(
            jnp.where(is_below & (my_col == panel_step), lower_full, current[:, :panel_width])
        )
    return current


def solution(mesh):
    placed = (P("prow", "pcol"), P(), P(), P())
    return jax.shard_map(
        body, mesh=mesh, in_specs=placed, out_specs=P("prow", "pcol"), check_vma=False
    )
```

profile of v0, /device:TPU:1, one launch (start us, length us, event | category | flops | bytes accessed | tf_op | source)
XLA Modules:
  0.0 605.7 jit_solution(10775062891973166959)
XLA Ops:
  6.5 4.8 copy.55
  11.5 5.8 gather_fusion
  17.3 3.1 copy.21
  20.4 1.8 copy.41
  22.2 4.8 broadcast_select_fusion.1
  27.2 116.5 %all-reduce.13.cloned.1.call-done = (f32[512,1024]{0,1:T(8,128)}, f32[512,1024]{0,1:T(8,128)}) async-done(((f32[512,1024]{0,1:T(8,128)}, f32[512,1024]{0,1:T(8,128)}), (f32[512,1024]{0,1:T(8,128)}, f32[512,1024]{0,1:T(8,128)})) %all-reduce.13.cloned.1.call-update) | async-done | bytes 4194320 | tf_op jit(solution)/shard_map/psum | solution.py:9
  143.7 1.9 copy.20
  145.6 6.4 %scatter_fusion = f32[1024,1024]{1,0:T(8,128)} fusion(f32[1024,1024]{1,0:T(8,128)} %copy.55, s32[512]{0:T(512)S(1)} %bitcast.54, f32[512,1024]{1,0:T(8,128)S(1)} %copy.20), kind=kCustom, calls=%fused_computation.2 | custom fusion | bytes 6293504 | tf_op jit(solution)/shard_map/scatter | solution.py:40
  152.0 5.4 copy.23
  157.4 8.1 %fusion.3 = (f32[1024,1024]{0,1:T(8,128)}, f32[512,1024]{0,1:T(8,128)S(1)}) fusion(f32[1024,1024]{0,1:T(8,128)} %copy.23, pred[]{:T(512)S(6)} %eq.59, f32[512,1024]{0,1:T(8,128)} %get-tuple-element.56, f32[2,512,512]{2,1,0:T(8,128)} %param.14, pred[1024]{0:T(1024)(128)(4,1)S(1)} %fusion.32), kind=kOutput, calls=%fused_computation.16 | convolution fusion | flops 3222274048 | bytes 11535361 | tf_op jit(solution)/shard_map/dot_general | solution.py:32
  165.5 3.2 slice_select_fusion.3
  168.9 0.6 compare_reduce_fusion
  169.6 114.8 %all-reduce.7.cloned.1.call-done = f32[1024,512]{0,1:T(8,128)} async-done(((f32[1024,512]{0,1:T(8,128)}), f32[1024,512]{0,1:T(8,128)}) %all-reduce.7.cloned.1.call-update) | async-done | bytes 2097168 | tf_op jit(solution)/shard_map/psum | solution.py:9
  284.3 5.5 fusion.11
  289.9 8.7 %convolution_subtract_fusion.1 = f32[1024,1024]{0,1:T(8,128)} fusion(f32[1024,1024]{0,1:T(8,128)S(1)} %copy-done, f32[512,1024]{0,1:T(8,128)S(1)} %get-tuple-element.67, f32[1024,512]{0,1:T(8,128)S(1)} %fusion.11, pred[1024]{0:T(1024)(128)(4,1)S(1)} %fusion.32, pred[1024]{0:T(1024)(128)(4,1)S(1)} %get-tuple-element.70), kind=kOutput, calls=%fused_computation.7 | convolution fusion | flops 6444548096 | bytes 12584960 | tf_op jit(solution)/shard_map/dot_general | solution.py:55
  298.6 3.9 fusion
  302.5 5.4 copy.27
  307.9 3.2 slice_select_fusion.2
  311.1 5.0 gather_fusion.1
  316.1 1.8 copy.30
  317.9 3.1 broadcast_select_fusion
  321.1 113.9 %all-reduce.11.cloned.1.call-done = (f32[512,1024]{0,1:T(8,128)}, f32[512,1024]{0,1:T(8,128)}) async-done(((f32[512,1024]{0,1:T(8,128)}, f32[512,1024]{0,1:T(8,128)}), (f32[512,1024]{0,1:T(8,128)}, f32[512,1024]{0,1:T(8,128)})) %all-reduce.11.cloned.1.call-update) | async-done | bytes 4194320 | tf_op jit(solution)/shard_map/psum | solution.py:9
  435.0 1.9 copy.28
  437.0 6.3 %scatter_fusion.1 = f32[1024,1024]{1,0:T(8,128)} fusion(f32[1024,1024]{1,0:T(8,128)} %copy.27, s32[512]{0:T(512)S(1)} %bitcast.55, f32[512,1024]{1,0:T(8,128)S(1)} %copy.28), kind=kCustom, calls=%fused_computation.3 | custom fusion | bytes 6293504 | tf_op jit(solution)/shard_map/scatter | solution.py:40
  443.3 5.3 copy.32
  448.6 8.0 %fusion.2 = (f32[1024,1024]{0,1:T(8,128)}, f32[512,1024]{0,1:T(8,128)S(1)}) fusion(f32[1024,1024]{0,1:T(8,128)} %copy.32, pred[]{:T(512)S(6)} %eq.64, f32[512,1024]{0,1:T(8,128)} %get-tuple-element.54, f32[2,512,512]{2,1,0:T(8,128)} %param.14, pred[1024]{0:T(1024)(128)(4,1)S(1)} %fusion.31), kind=kOutput, calls=%fused_computation.12 | convolution fusion | flops 3222274048 | bytes 11535361 | tf_op jit(solution)/shard_map/dot_general | solution.py:32
  456.7 3.2 slice_select_fusion
  459.9 115.7 %all-reduce.9.cloned.1.call-done = f32[1024,512]{0,1:T(8,128)} async-done(((f32[1024,512]{0,1:T(8,128)}), f32[1024,512]{0,1:T(8,128)}) %all-reduce.9.cloned.1.call-update) | async-done | bytes 2097168 | tf_op jit(solution)/shard_map/psum | solution.py:9
  575.6 5.5 fusion.8
  581.1 8.7 %convolution_subtract_fusion = f32[1024,1024]{0,1:T(8,128)} fusion(f32[1024,1024]{0,1:T(8,128)S(1)} %copy-done.1, f32[512,1024]{0,1:T(8,128)S(1)} %get-tuple-element.69, f32[1024,512]{0,1:T(8,128)S(1)} %fusion.8, pred[1024]{0:T(1024)(128)(4,1)S(1)} %fusion.31, pred[1024]{0:T(1024)(128)(4,1)S(1)} %fusion.33), kind=kOutput, calls=%fused_computation.6 | convolution fusion | flops 6444548096 | bytes 12584960 | tf_op jit(solution)/shard_map/dot_general | solution.py:55
  589.9 3.9 fusion.1
  593.8 5.3 copy.36
  (30 shorter events, 0.6 us)
Async XLA Ops:
  6.5 4.8 copy-start.2
  6.5 137.2 %all-reduce.13.cloned.1.call-start = ((), (), s32[]{:S(2)}) async-start(), calls=%async_computation.3 | async-start | bytes 8388608 | tf_op jit(solution)/shard_map/psum | solution.py:9
  17.3 3.1 slice-start
  27.1 257.3 %all-reduce.7.cloned.1.call-start = ((), (), s32[]{:S(2)}) async-start(), calls=%async_computation | async-start | bytes 4194304 | tf_op jit(solution)/shard_map/psum | solution.py:9
  168.7 266.4 %all-reduce.11.cloned.1.call-start = ((), (), s32[]{:S(2)}) async-start(), calls=%async_computation.2 | async-start | bytes 8388608 | tf_op jit(solution)/shard_map/psum | solution.py:9
  284.3 5.5 copy-start
  321.1 254.5 %all-reduce.9.cloned.1.call-start = ((), (), s32[]{:S(2)}) async-start(), calls=%async_computation.1 | async-start | bytes 4194304 | tf_op jit(solution)/shard_map/psum | solution.py:9
  575.6 5.5 copy-start.1
Sparse Core Ops, SparseCore 0:
  27.2 116.4 all-reduce.12
  168.8 115.4 all-reduce.6
  321.2 113.8 all-reduce.10
  460.0 115.5 all-reduce.8
where the time goes:
time: 606 us
  waiting for transfers between devices  461 us (76%)
  local copies, waits for them, and re-layouts  60.3 us (10%)
  matrix products  44.6 us (7%)
  other arithmetic  26.2 us (4%)
  between operations  13.3 us (2%)
    psum x4, waiting for transfers between devices, spread(): return lax.psum(kept, axis)  461 us
    scatter x4, local copies, waits for them, and re-layouts, body(): current = current.at[dropped_slot].set(old_top, mode='drop')  23.4 us
    dot_general x2, matrix products, body(): jnp.dot(lower_part, upper_part, precision=lax.Precision.HIGHEST, preferre...  17.5 us
    dot_general x2, matrix products, body(): jnp.dot(inverse_lower, new_top, precision=lax.Precision.HIGHEST, preferre...  16.1 us
    gather x4, local copies, waits for them, and re-layouts, body(): picked = jnp.where(is_mine[:, None], current[local_slot], 0.0)  15.7 us
  transfers between devices with their start and end apart: 4, of which 4 were waited for; matrix products, arithmetic and copies ran while one was open for 0% of the time, Pallas kernels for 0%

commit v1 on v0

--- a/solution.py
+++ b/solution.py
@@ -6,7 +6,7 @@
 
 def spread(value, axis, source):
     kept = jnp.where(lax.axis_index(axis) == source, value, 0).astype(value.dtype)
-    return lax.psum(kept, axis)
+    return jnp.sum(lax.all_gather(kept, axis), axis=0)
 
 
 def body(matrix, pivots, lower_inverses, upper_inverses):

time: 606 us -> 1140 us (1.88)
  waiting for transfers between devices: 461 us -> 817 us
  local copies, waits for them, and re-layouts: 60.3 us -> 198 us
  other arithmetic: 26.2 us -> 60.7 us
    all_gather x0 -> x4, waiting for transfers between devices: none -> 728 us  [spread(): return jnp.sum(lax.all_gather(kept, axis), axis=0)]
    psum x4 -> x2, waiting for transfers between devices: 461 us -> 89.1 us  [body(): new_top = lax.psum(picked, 'prow')]
    unnamed x8 -> x14, local copies, waits for them, and re-layouts: 6.65 us -> 144 us
    reduce_sum x0 -> x4, other arithmetic: none -> 36.7 us  [spread(): return jnp.sum(lax.all_gather(kept, axis), axis=0)]
  transfers between devices with their start and end apart: 4 -> 6, of which waited for: 4 -> 6; matrix products, arithmetic and copies ran while one was open for 0% -> 13% of each run, Pallas kernels for 0% -> 0%
where the time goes in v1:
time: 1140 us; the launch traced here: 1130 us
  waiting for transfers between devices  817 us (72%)
  local copies, waits for them, and re-layouts  198 us (17%)
  other arithmetic  60.7 us (5%)
  matrix products  41.7 us (4%)
  between operations  14.2 us (1%)
    all_gather x4, waiting for transfers between devices, spread(): return jnp.sum(lax.all_gather(kept, axis), axis=0)  728 us
    unnamed x14, local copies, waits for them, and re-layouts  144 us
    psum x2, waiting for transfers between devices, body(): new_top = lax.psum(picked, 'prow')  89.1 us
    reduce_sum x4, other arithmetic, spread(): return jnp.sum(lax.all_gather(kept, axis), axis=0)  36.7 us
    scatter x4, local copies, waits for them, and re-layouts, body(): current = current.at[dropped_slot].set(old_top, mode='drop')  24 us
  transfers between devices with their start and end apart: 6, of which 6 were waited for; matrix products, arithmetic and copies ran while one was open for 13% of the time, Pallas kernels for 0%

profile of v1, /device:TPU:1, one launch (start us, length us, event | category | flops | bytes accessed | tf_op | source)
XLA Modules:
  0.0 1132.4 jit_solution(6810927491885352956)
XLA Ops:
  6.5 4.8 copy.70
  18.7 5.0 gather_fusion
  28.8 193.3 %all-gather.9.cloned.1.call-done = f32[8192,1024]{0,1:T(8,128)} async-done(((f32[512,1024]{0,1:T(8,128)}), f32[8192,1024]{0,1:T(8,128)}) %all-gather.9.cloned.1.call-update) | async-done | bytes 33554448 | tf_op jit(solution)/shard_map/all_gather | solution.py:9
  222.1 34.9 %copy.57 = f32[128,8,16,512]{3,2,1,0:T(8,128)S(1)} copy(f32[128,8,16,512]{3,1,2,0:T(8,128)} %bitcast.74) | data formatting | bytes 67108864
  257.0 9.7 bitcast_reduce_fusion.3
  268.7 6.6 scatter_fusion
  275.3 5.4 copy.38
  280.7 44.6 %all-reduce.3.cloned.1.call-done = f32[512,1024]{0,1:T(8,128)} async-done(((f32[512,1024]{0,1:T(8,128)}), f32[512,1024]{0,1:T(8,128)}) %all-reduce.3.cloned.1.call-update) | async-done | bytes 2097168 | tf_op jit(solution)/shard_map/psum | solution.py:31
  325.3 8.1 fusion.3
  337.4 175.1 %all-gather.11.cloned.1.call-done = f32[16384,512]{0,1:T(8,128)} async-done(((f32[1024,512]{0,1:T(8,128)}), f32[16384,512]{0,1:T(8,128)}) %all-gather.11.cloned.1.call-update) | async-done | bytes 33554448 | tf_op jit(solution)/shard_map/all_gather | solution.py:9
  512.5 32.5 %copy.58 = f32[64,8,16,1024]{3,2,1,0:T(8,128)S(1)} copy(f32[64,8,16,1024]{3,1,2,0:T(8,128)} %bitcast.76) | data formatting | bytes 67108864
  545.0 8.8 bitcast_reduce_fusion.2
  553.8 4.9 fusion.11
  558.7 7.0 convolution_subtract_fusion.1
  570.9 5.6 copy.42
  576.5 5.0 gather_fusion.1
  583.3 3.4 broadcast_select_fusion
  586.8 184.1 %all-gather.13.cloned.1.call-done = f32[8192,1024]{0,1:T(8,128)} async-done(((f32[512,1024]{0,1:T(8,128)}), f32[8192,1024]{0,1:T(8,128)}) %all-gather.13.cloned.1.call-update) | async-done | bytes 33554448 | tf_op jit(solution)/shard_map/all_gather | solution.py:9
  770.9 34.9 %copy.59 = f32[128,8,16,512]{3,2,1,0:T(8,128)S(1)} copy(f32[128,8,16,512]{3,1,2,0:T(8,128)} %bitcast.75) | data formatting | bytes 67108864
  805.8 9.7 bitcast_reduce_fusion.1
  817.4 6.5 scatter_fusion.1
  823.9 5.5 copy.47
  829.4 44.5 %all-reduce.5.cloned.1.call-done = f32[512,1024]{0,1:T(8,128)} async-done(((f32[512,1024]{0,1:T(8,128)}), f32[512,1024]{0,1:T(8,128)}) %all-reduce.5.cloned.1.call-update) | async-done | bytes 2097168 | tf_op jit(solution)/shard_map/psum | solution.py:31
  873.9 8.0 fusion.2
  881.9 3.2 slice_select_fusion
  885.2 175.8 %all-gather.15.cloned.1.call-done = f32[16384,512]{0,1:T(8,128)} async-done(((f32[1024,512]{0,1:T(8,128)}), f32[16384,512]{0,1:T(8,128)}) %all-gather.15.cloned.1.call-update) | async-done | bytes 33554448 | tf_op jit(solution)/shard_map/all_gather | solution.py:9
  1061.0 32.5 %copy.60 = f32[64,8,16,1024]{3,2,1,0:T(8,128)S(1)} copy(f32[64,8,16,1024]{3,1,2,0:T(8,128)} %bitcast.77) | data formatting | bytes 67108864
  1093.5 8.6 bitcast_reduce_fusion
  1102.2 4.9 fusion.8
  1107.1 8.7 convolution_subtract_fusion
  1115.8 4.0 fusion.1
  1119.8 5.3 copy.51
  (48 shorter events, 27.3 us)
Async XLA Ops:
  6.5 215.6 %all-gather.9.cloned.1.call-start = ((), (), s32[]{:S(2)}) async-start(), calls=%async_computation.2 | async-start | bytes 35651584 | tf_op jit(solution)/shard_map/all_gather | solution.py:9
  11.3 1.6 slice-start
  17.9 0.7 copy-start.3
  18.0 307.3 %all-reduce.3.cloned.1.call-start = ((), (), s32[]{:S(2)}) async-start(), calls=%async_computation | async-start | bytes 4194304 | tf_op jit(solution)/shard_map/psum | solution.py:31
  28.7 483.7 %all-gather.11.cloned.1.call-start = ((), (), s32[]{:S(2)}) async-start(), calls=%async_computation.3 | async-start | bytes 35651584 | tf_op jit(solution)/shard_map/all_gather | solution.py:9
  336.6 434.3 %all-gather.13.cloned.1.call-start = ((), (), s32[]{:S(2)}) async-start(), calls=%async_computation.4 | async-start | bytes 35651584 | tf_op jit(solution)/shard_map/all_gather | solution.py:9
  553.8 4.9 copy-start
  567.1 2.0 copy-start.2
  570.8 303.1 %all-reduce.5.cloned.1.call-start = ((), (), s32[]{:S(2)}) async-start(), calls=%async_computation.1 | async-start | bytes 4194304 | tf_op jit(solution)/shard_map/psum | solution.py:31
  586.7 474.3 %all-gather.15.cloned.1.call-start = ((), (), s32[]{:S(2)}) async-start(), calls=%async_computation.5 | async-start | bytes 35651584 | tf_op jit(solution)/shard_map/all_gather | solution.py:9
  1102.2 4.9 copy-start.1
Sparse Core Ops, SparseCore 0:
  18.1 204.0 all-gather.8
  225.4 99.7 all-reduce.2
  336.8 175.6 all-gather.10
  570.9 199.9 all-gather.12
  774.1 99.7 all-reduce.4
  885.3 175.6 all-gather.14
